TPU v7x, 32 devices: a whole 2x2x4 slice. The times are simulated.
32 devices in a mesh: seq: 2 (over x), mp: 4 (over y, core), dp: 4 (over z).
Axes of the slice: x: 2, y: 2, z: 4, core: 2. Of those that a mesh axis runs over, the one named last changes fastest.
Arguments:
- tokens: bfloat16 [16384, 2048], P(('dp', 'seq'), 'mp'), parts along dimension 0, may hold values from -6 to 6
- w_query: bfloat16 [2048, 2048], P(None, 'mp'), may hold values from -0.125 to 0.125
- w_key: bfloat16 [2048, 2048], P(None, 'mp'), may hold values from -0.125 to 0.125
- w_value: bfloat16 [2048, 2048], P(None, 'mp'), may hold values from -0.125 to 0.125
- w_gate: bfloat16 [2048, 2048], P(None, 'mp'), may hold values from -0.125 to 0.125
- decay_exponent: int32 [16], P('mp'), may hold values from 5 to 16
- forget: float32 [16384, 16], P(('dp', 'seq'), 'mp'), parts along dimension 0, may hold values from 0 to 0.69
- norm_gain: float32 [2048], replicated, may hold values from 0.1 to 1.9
Outputs:
- retained: bfloat16 [16384, 2048], P(('dp', 'seq', 'mp')), parts along dimension 0
There are 4 independent parts, one for each index of `dp`. A program takes and returns all parts, laid end to end along the dimension named above; an argument that names none is the same for every part. Nothing has to cross between parts.
All inputs are finite; a program needn't handle non-finite values.
Results may differ from a plain program's by a relative error of at most 0.015.
Values may be sent and summed in bfloat16 or wider, within the bound.
No kernel may reach another device: no remote copies, remote signals or barrier semaphores. Data moves between devices by JAX's collectives and lax.ppermute only.
A program may use at most 64 MiB of HBM per device.

v0:
```python
import jax
import jax.numpy as jnp
from jax import lax
from jax.sharding import PartitionSpec as P

DH = 128


def carried_in(shard, axis, join, neutral):
    place = lax.axis_index(axis)
    gathered = jax.tree.map(
        lambda a, kind: lax.all_gather(a.astype(kind), axis), shard, (jnp.bfloat16, jnp.bfloat16)
    )
    state = jax.tree.map(lambda a, e: jnp.zeros_like(a) + jnp.asarray(e, a.dtype), shard, neutral)

    def one(hop, state):
        return join(
            state,
            jax.tree.map(
                lambda a, own: lax.dynamic_index_in_dim(a, hop, 0, False).astype(own.dtype),
                gathered,
                shard,
            ),
        )

    return lax.fori_loop(0, place, one, state)


def run_blocks(queries, key_rows, values, logdecay, head_count, head_width):
    seq_rows = queries.shape[0]
    block_rows = 512
    block_count = seq_rows // block_rows

    def shaped(source):
        return source.reshape(block_count, block_rows, head_count, head_width)

    decays = logdecay.reshape(block_count, block_rows, head_count)
    position = lax.broadcasted_iota(jnp.int32, (block_rows, block_rows), 0)
    earlier = lax.broadcasted_iota(jnp.int32, (block_rows, block_rows), 1)
    causal = position >= earlier

    def advance(carried, pieces):
        kv_state, offset = carried
        query_blk, key_blk, value_blk, decay_blk = pieces
        running = jnp.cumsum(decay_blk, axis=0)
        heads_first = running.T
        log_gap = heads_first[:, :, None] - heads_first[:, None, :]
        decay_mask = jnp.where(causal[None], jnp.exp(jnp.where(causal[None], log_gap, 0.0)), 0.0)
        scores = jnp.einsum("tha,sha->hts", query_blk, key_blk, preferred_element_type=jnp.float32)
        scores = (scores * decay_mask).astype(jnp.bfloat16)
        inner = jnp.einsum("hts,shb->thb", scores, value_blk, preferred_element_type=jnp.float32)
        query_float = query_blk.astype(jnp.float32)
        earlier_part = jnp.einsum(
            "tha,hab->thb",
            query_float * jnp.exp(running)[:, :, None],
            kv_state,
            precision=lax.Precision.HIGHEST,
        )
        query_device = query_float * jnp.exp(running + offset[None, :])[:, :, None]
        key_scaled = key_blk.astype(jnp.float32) * jnp.exp(running[-1:] - running)[:, :, None]
        kv_state = jnp.exp(running[-1])[:, None, None] * kv_state + jnp.einsum(
            "sha,shb->hab",
            key_scaled,
            value_blk.astype(jnp.float32),
            precision=lax.Precision.HIGHEST,
        )
        return ((kv_state, offset + running[-1]), (inner + earlier_part, query_device))

    initial = (
        jnp.zeros((head_count, head_width, head_width), jnp.float32),
        jnp.zeros((head_count,), jnp.float32),
    )
    final, outputs = lax.scan(
        advance, initial, (shaped(queries), shaped(key_rows), shaped(values), decays)
    )
    local_part = outputs[0].reshape(seq_rows, head_count, head_width)
    query_device = outputs[1].reshape(seq_rows, head_count, head_width)
    return (local_part, query_device, final[0], final[1])


def combine_states(before, after):
    return (before[0] * after[0], after[0][:, None, None] * before[1] + after[1])


def body(tokens, w_query, w_key, w_value, w_gate, decay_exponent, forget, norm_gain):
    seq_rows = tokens.shape[0]
    local_width = w_query.shape[1]
    head_count = decay_exponent.shape[0]
    head_width = local_width // head_count
    empty = jnp.zeros((seq_rows, local_width), jnp.float32)
    summed = (empty, empty, empty, empty)
    piece = lax.all_gather(tokens, "mp", axis=1, tiled=True)
    results = []
    for weight, partial_value in zip((w_query, w_key, w_value, w_gate), summed):
        results.append(jnp.dot(piece, weight, preferred_element_type=jnp.float32))
    projected = tuple(results)
    queries = projected[0].astype(jnp.bfloat16)
    key_rows = (projected[1] * DH ** (-0.5)).astype(jnp.bfloat16)
    values = projected[2].astype(jnp.bfloat16)
    gate = projected[3].astype(jnp.bfloat16)
    rate = jnp.log1p(-jnp.exp2(-decay_exponent.astype(jnp.float32)))
    logdecay = rate[None, :] - forget
    local_part, query_device, own_state, own_total = run_blocks(
        queries, key_rows, values, logdecay, head_count, head_width
    )
    prefix = carried_in(
        (jnp.exp(own_total), own_state),
        "seq",
        combine_states,
        (jnp.ones_like(own_total), jnp.zeros_like(own_state)),
    )
    incoming = prefix[1]
    from_before = jnp.einsum(
        "tha,hab->thb", query_device, incoming, precision=lax.Precision.HIGHEST
    )
    output = (local_part + from_before).astype(jnp.bfloat16).reshape(seq_rows, local_width)
    moved_output, moved_gate = (
        lax.all_to_all(output, "mp", split_axis=0, concat_axis=1, tiled=True),
        lax.all_to_all(gate, "mp", split_axis=0, concat_axis=1, tiled=True),
    )
    output_float = moved_output.astype(jnp.float32)
    rstd = lax.rsqrt(jnp.mean(output_float * output_float, axis=1) + 1e-06)
    gated = (
        jax.nn.silu(moved_gate.astype(jnp.float32))
        * output_float
        * rstd[:, None]
        * norm_gain[None, :]
    )
    return gated.astype(jnp.bfloat16)


def solution(mesh):
    placed = (
        P(("dp", "seq"), "mp"),
        P(None, "mp"),
        P(None, "mp"),
        P(None, "mp"),
        P(None, "mp"),
        P("mp"),
        P(("dp", "seq"), "mp"),
        P(),
    )
    return jax.shard_map(
        body, mesh=mesh, in_specs=placed, out_specs=P(("dp", "seq", "mp"), None), check_vma=False
    )
```

profile of v0, /device:TPU:0, one launch (start us, length us, event | category | flops | bytes accessed | tf_op | source)
XLA Modules:
  0.0 337.5 jit_solution(5486481289894038509)
XLA Ops:
  10.7 59.2 %all-gather.4.cloned.1.call-done = bf16[2048,2048]{1,0:T(8,128)(2,1)} async-done(((bf16[2048,512]{1,0:T(8,128)(2,1)}), bf16[2048,2048]{1,0:T(8,128)(2,1)}) %all-gather.4.cloned.1.call-update) | async-done | bytes 8388624 | tf_op jit(solution)/shard_map/all_gather | solution.py:92
  69.9 9.1 %convolution_convert_fusion = bf16[2048,512]{1,0:T(8,128)(2,1)} fusion(bf16[2048,2048]{1,0:T(8,128)(2,1)} %all-gather.4.cloned.1.call-done, bf16[2048,512]{1,0:T(8,128)(2,1)S(1)} %copy-done), kind=kOutput, calls=%fused_computation.48 | convolution fusion | flops 4296015872 | bytes 12582912 | tf_op jit(solution)/shard_map/dot_general | solution.py:95
  79.0 4.0 %reshape.90 = bf16[4,512,4,128]{3,2,1,0:T(4,128)(2,1)} reshape(bf16[2048,512]{1,0:T(8,128)(2,1)} %convolution_convert_fusion) | data formatting | bytes 4194304 | tf_op jit(solution)/shard_map/reshape | solution.py:35
  83.0 8.5 %convolution_convert_fusion.1 = bf16[2048,512]{1,0:T(8,128)(2,1)S(1)} fusion(bf16[2048,2048]{1,0:T(8,128)(2,1)} %all-gather.4.cloned.1.call-done, bf16[2048,512]{1,0:T(8,128)(2,1)} %param.15), kind=kOutput, calls=%fused_computation.49 | convolution fusion | flops 4296015872 | bytes 12582912 | tf_op jit(solution)/shard_map/dot_general | solution.py:95
  91.5 2.1 reshape.89
  93.6 8.5 %multiply_convert_fusion.2 = bf16[2048,512]{1,0:T(8,128)(2,1)S(1)} fusion(bf16[2048,2048]{1,0:T(8,128)(2,1)} %all-gather.4.cloned.1.call-done, bf16[2048,512]{1,0:T(8,128)(2,1)} %param.14), kind=kOutput, calls=%fused_computation.47 | convolution fusion | flops 4297064448 | bytes 12582912 | tf_op jit(solution)/shard_map/dot_general | solution.py:95
  102.1 2.0 reshape.88
  104.1 137.0 %while.31 = (s32[]{:T(128)}, f32[4,128,128]{2,1,0:T(8,128)S(1)}, f32[4]{0:T(128)S(1)}, f32[4,512,4,128]{1,0,3,2:T(4,128)}, f32[4,512,4,128]{3,1,0,2:T(8,128)}, /...) while((s32[]{:T(128)}, f32[4,128,128]{2,1,0:T(8,128)S(1)}, ...), condition=%wide.region_3.4_spmd.clone.clone, body=%wide.region_0.3_spmd.clone.clone.sunk | while | flops 1350045696 | bytes 18760368 | solution.py:73
  109.1 2.0 fusion.48
  112.5 2.4 convolution_add_fusion.2
  116.0 21.0 %dynamic_update_slice.15 = f32[4,512,4,128]{1,0,3,2:T(4,128)} dynamic-update-slice(f32[4,512,4,128]{1,0,3,2:T(4,128)} %get-tuple-element.371, f32[1,512,4,128]{1,0,3,2:T(1,128)S(1)} %copy.143, s32[]{:T(128)S(6)} %copy.151, s32[]{:T(128)} %constant.52.clone.1..sunk.1, s32[]{:T(128)} %constant.52.clone.1..sunk.1, s32[]{:T(128)} %constant.52.clone.1..sunk.1) | dynamic-update-slice | bytes 2097156 | tf_op jit(solution)/shard_map/while/body/jit(dynamic_update_index_in_dim)/dynamic_update_slice | solution.py:73
  146.7 2.4 convolution_add_fusion.2
  150.2 21.0 %dynamic_update_slice.15 = f32[4,512,4,128]{1,0,3,2:T(4,128)} dynamic-update-slice(f32[4,512,4,128]{1,0,3,2:T(4,128)} %get-tuple-element.371, f32[1,512,4,128]{1,0,3,2:T(1,128)S(1)} %copy.143, s32[]{:T(128)S(6)} %copy.151, s32[]{:T(128)} %constant.52.clone.1..sunk.1, s32[]{:T(128)} %constant.52.clone.1..sunk.1, s32[]{:T(128)} %constant.52.clone.1..sunk.1) | dynamic-update-slice | bytes 2097156 | tf_op jit(solution)/shard_map/while/body/jit(dynamic_update_index_in_dim)/dynamic_update_slice | solution.py:73
  177.6 2.0 fusion.48
  181.0 2.4 convolution_add_fusion.2
  184.5 21.0 %dynamic_update_slice.15 = f32[4,512,4,128]{1,0,3,2:T(4,128)} dynamic-update-slice(f32[4,512,4,128]{1,0,3,2:T(4,128)} %get-tuple-element.371, f32[1,512,4,128]{1,0,3,2:T(1,128)S(1)} %copy.143, s32[]{:T(128)S(6)} %copy.151, s32[]{:T(128)} %constant.52.clone.1..sunk.1, s32[]{:T(128)} %constant.52.clone.1..sunk.1, s32[]{:T(128)} %constant.52.clone.1..sunk.1) | dynamic-update-slice | bytes 2097156 | tf_op jit(solution)/shard_map/while/body/jit(dynamic_update_index_in_dim)/dynamic_update_slice | solution.py:73
  215.2 2.4 convolution_add_fusion.2
  218.7 21.0 %dynamic_update_slice.15 = f32[4,512,4,128]{1,0,3,2:T(4,128)} dynamic-update-slice(f32[4,512,4,128]{1,0,3,2:T(4,128)} %get-tuple-element.371, f32[1,512,4,128]{1,0,3,2:T(1,128)S(1)} %copy.143, s32[]{:T(128)S(6)} %copy.151, s32[]{:T(128)} %constant.52.clone.1..sunk.1, s32[]{:T(128)} %constant.52.clone.1..sunk.1, s32[]{:T(128)} %constant.52.clone.1..sunk.1) | dynamic-update-slice | bytes 2097156 | tf_op jit(solution)/shard_map/while/body/jit(dynamic_update_index_in_dim)/dynamic_update_slice | solution.py:73
  241.4 9.8 %convolution_convert_fusion.2 = bf16[2048,512]{1,0:T(8,128)(2,1)} fusion(bf16[2048,2048]{1,0:T(8,128)(2,1)} %all-gather.4.cloned.1.call-done, bf16[2048,512]{1,0:T(8,128)(2,1)} %param.16), kind=kOutput, calls=%fused_computation.50 | convolution fusion | flops 4296015872 | bytes 12582912 | tf_op jit(solution)/shard_map/dot_general | solution.py:95
  251.2 4.4 %all-to-all-start = ((bf16[4,512,512]{2,1,0:T(8,128)(2,1)}), bf16[4,512,512]{2,1,0:T(8,128)(2,1)}, u32[]{:S(2)}, u32[]{:S(2)}) async-start(bf16[4,512,512]{2,1,0:T(8,128)(2,1)} %bitcast.2), calls=%async_computation | async-start | bytes 4194304 | tf_op jit(solution)/shard_map/all_to_all | solution.py:119
  255.7 4.9 %all-reduce = bf16[8]{0:T(256)(128)(2,1)S(1)} all-reduce(bf16[8]{0:T(256)(128)(2,1)S(1)} %dynamic-update-slice), channel_id=2, replica_groups=mesh['seq'=2,'mp'=4,'dp'=4] {'seq'}, use_global_device_ids=true, to_apply=%add | all-reduce | flops 8 | bytes 32
  260.7 5.7 %all-gather.1 = bf16[8,128,128]{2,1,0:T(8,128)(2,1)S(1)} all-gather(bf16[4,128,128]{2,1,0:T(8,128)(2,1)S(1)} %convert_element_type.89), channel_id=3, replica_groups=mesh['seq'=2,'mp'=4,'dp'=4] {'seq'}, dimensions={0}, use_global_device_ids=true | all-gather | bytes 393216 | tf_op jit(solution)/shard_map/all_gather | solution.py:12
  266.4 6.1 %reshape.91 = f32[2048,4,128]{0,2,1:T(8,128)} reshape(f32[4,512,4,128]{1,0,3,2:T(4,128)} %get-tuple-element.107) | data formatting | bytes 8388608 | tf_op jit(solution)/shard_map/reshape | solution.py:76
  272.5 8.8 %fusion.24 = bf16[2048,4,128]{0,2,1:T(8,128)(2,1)} fusion(f32[2048,4,128]{0,2,1:T(8,128)} %reshape.91, f32[4,128,128]{2,1,0:T(8,128)S(1)} %get-tuple-element.110, f32[2048,4,128]{2,0,1:T(8,128)} %bitcast.128), kind=kOutput, calls=%fused_computation.43 | convolution fusion | flops 1612709888 | bytes 10747904 | tf_op jit(solution)/shard_map/tha,hab->thb/dot_general | solution.py:113
  281.4 3.3 all_to_all.22
  286.4 3.6 %all-to-all-start.1 = ((bf16[4,512,512]{1,2,0:T(8,128)(2,1)}), bf16[4,512,512]{1,2,0:T(8,128)(2,1)S(1)}, u32[]{:S(2)}, u32[]{:S(2)}) async-start(bf16[4,512,512]{1,2,0:T(8,128)(2,1)} %copy.79), calls=%async_computation.1 | async-start | bytes 4194304 | tf_op jit(solution)/shard_map/all_to_all | solution.py:118
  290.0 2.2 convert_bitcast_fusion
  292.2 2.6 copy.94
  294.8 20.9 %all-to-all-done.1 = bf16[4,512,512]{1,2,0:T(8,128)(2,1)S(1)} async-done(((bf16[4,512,512]{1,2,0:T(8,128)(2,1)}), bf16[4,512,512]{1,2,0:T(8,128)(2,1)S(1)}, u32[]{:S(2)}, u32[]{:S(2)}) %all-to-all-start.1) | async-done | bytes 2097184 | tf_op jit(solution)/shard_map/all_to_all | solution.py:118
  316.2 2.6 convert_element_type.105
  318.8 5.4 %copy.80 = f32[512,2048]{1,0:T(8,128)} copy(f32[512,2048]{0,1:T(8,128)} %bitcast.127) | data formatting | bytes 8388608 | tf_op jit(solution)/shard_map/convert_element_type | solution.py:121
  324.2 6.4 %multiply_convert_fusion.1 = bf16[512,2048]{1,0:T(8,128)(2,1)} fusion(f32[512,2048]{1,0:T(8,128)} %copy.80, f32[512,2048]{1,0:T(8,128)} %bitcast.126, f32[2048]{0:T(1024)S(1)} %copy-done.3, f32[512]{0:T(512)S(1)} %add_rsqrt_fusion), kind=kLoop, calls=%fused_computation.45 | loop fusion | flops 8388608 | bytes 10496000 | tf_op jit(solution)/shard_map/convert_element_type | solution.py:129
  (100 shorter events, 45.1 us)
Async XLA Ops:
  6.5 63.4 %copy-start = (bf16[2048,512]{1,0:T(8,128)(2,1)S(1)}, bf16[2048,512]{1,0:T(8,128)(2,1)}, u32[]{:S(2)}) copy-start(bf16[2048,512]{1,0:T(8,128)(2,1)} %param.13) | copy-start | bytes 6291460
  6.5 63.4 %all-gather.4.cloned.1.call-start = ((), (), s32[]{:S(2)}) async-start(), calls=%async_computation.2 | async-start | bytes 10485760 | tf_op jit(solution)/shard_map/all_gather | solution.py:92
  107.4 1.8 copy-start.2
  141.6 1.8 copy-start.2
  175.9 1.8 copy-start.2
  210.1 1.8 copy-start.2
  251.2 35.2 %all-to-all-start = ((bf16[4,512,512]{2,1,0:T(8,128)(2,1)}), bf16[4,512,512]{2,1,0:T(8,128)(2,1)}, u32[]{:S(2)}, u32[]{:S(2)}) async-start(bf16[4,512,512]{2,1,0:T(8,128)(2,1)} %bitcast.2), calls=%async_computation | async-start | bytes 4194304 | tf_op jit(solution)/shard_map/all_to_all | solution.py:119
  286.4 29.3 %all-to-all-start.1 = ((bf16[4,512,512]{1,2,0:T(8,128)(2,1)}), bf16[4,512,512]{1,2,0:T(8,128)(2,1)S(1)}, u32[]{:S(2)}, u32[]{:S(2)}) async-start(bf16[4,512,512]{1,2,0:T(8,128)(2,1)} %copy.79), calls=%async_computation.1 | async-start | bytes 4194304 | tf_op jit(solution)/shard_map/all_to_all | solution.py:118
  318.8 5.4 %copy-start.3 = (f32[2048]{0:T(1024)S(1)}, f32[2048]{0:T(1024)}, u32[]{:S(2)}) copy-start(f32[2048]{0:T(1024)} %param.19) | copy-start | bytes 24580
  324.2 6.4 %copy-start.1 = (bf16[2048,512]{1,0:T(8,128)(2,1)S(1)}, bf16[2048,512]{1,0:T(8,128)(2,1)}, u32[]{:S(2)}) copy-start(bf16[2048,512]{1,0:T(8,128)(2,1)} %param.13) | copy-start | bytes 6291460
Sparse Core Ops, SparseCore 0:
  8.9 60.9 all-gather.3
where the time goes:
time: 341 us; the launch traced here: 337 us
  local copies, waits for them, and re-layouts  131 us (38%)
  waiting for transfers between devices  80.8 us (24%)
  matrix products  67.6 us (20%)
  other arithmetic  25.1 us (7%)
  between operations  14.2 us (4%)
  blocking collectives  10.7 us (3%)
  starting transfers between devices  8.06 us (2%)
    dynamic_update_slice x8, local copies, waits for them, and re-layouts, run_blocks(): lax.scan(advance, initial, (shaped(queries), shaped(key_rows), shaped(val...  88.5 us
    all_gather x1, waiting for transfers between devices, body(): piece = lax.all_gather(tokens, 'mp', axis=1, tiled=True)  59.2 us
    dot_general x4, matrix products, body(): results.append(jnp.dot(piece, weight, preferred_element_type=jnp.float32))  35.9 us
    all_to_all x1, waiting for transfers between devices, body(): lax.all_to_all(output, 'mp', split_axis=0, concat_axis=1, tiled=True)  20.9 us
    dynamic_slice x8, local copies, waits for them, and re-layouts, run_blocks(): lax.scan(advance, initial, (shaped(queries), shaped(key_rows), shaped(val...  11.9 us
    dot_general x4, matrix products, advance(): jnp.einsum('sha,shb->hab', key_scaled, value_blk.astype(jnp.float32), pre...  9.56 us
    dot_general x1, matrix products, body(): jnp.einsum('tha,hab->thb', query_device, incoming, precision=lax.Precisio...  8.83 us
    reshape x3, local copies, waits for them, and re-layouts, shaped(): return source.reshape(block_count, block_rows, head_count, head_width)  8.09 us
  transfers between devices with their start and end apart: 3, of which 2 were waited for; matrix products, arithmetic and copies ran while one was open for 7% of the time, Pallas kernels for 0%

commit v1 on v0

v1 whole, which is shorter than its diff:
```python
import functools

import jax
import jax.numpy as jnp
from jax import lax
from jax.experimental import pallas as pl
from jax.experimental.pallas import tpu as pltpu
from jax.sharding import PartitionSpec as P

DH = 128


def block_of(rows, most):
    block = min(rows, most)
    while rows % block:
        block //= 2
    return block


def running_sum(decay_rows):
    width = decay_rows.shape[1]
    upto = (
        lax.broadcasted_iota(jnp.int32, (width, width), 0)
        <= lax.broadcasted_iota(jnp.int32, (width, width), 1)
    ).astype(jnp.float32)
    return jnp.dot(
        decay_rows, upto, precision=lax.Precision.HIGHEST, preferred_element_type=jnp.float32
    )


def next_state(state, key_blk, value_blk, column, last):
    scaled = (key_blk.astype(jnp.float32) * jnp.exp(last - column)).astype(jnp.bfloat16)
    return jnp.exp(last) * state + lax.dot_general(
        scaled, value_blk, (((0,), (0,)), ((), ())), preferred_element_type=jnp.float32
    )


def state_kernel(decay_ref, key_ref, value_ref, state_ref, total_ref, *, heads, width):
    @pl.when(pl.program_id(0) == 0)
    def _():
        state_ref[...] = jnp.zeros_like(state_ref)
        total_ref[...] = jnp.zeros_like(total_ref)

    running = running_sum(decay_ref[...])
    columns = running.T
    last_at = running.shape[1] - 1
    for h in range(heads):
        at = slice(h * width, (h + 1) * width)
        last = running[h : h + 1, last_at:]
        state_ref[h] = next_state(
            state_ref[h], key_ref[:, at], value_ref[:, at], columns[:, h : h + 1], last
        )
    total_ref[...] += jnp.broadcast_to(running[:, last_at:], total_ref.shape)


def retain_kernel(
    decay_ref, query_ref, key_ref, value_ref, initial_ref, out_ref, state_ref, *, heads, width
):
    @pl.when(pl.program_id(0) == 0)
    def _():
        state_ref[...] = initial_ref[...]

    running = running_sum(decay_ref[...])
    columns = running.T
    size = running.shape[1]
    causal = lax.broadcasted_iota(jnp.int32, (size, size), 0) >= lax.broadcasted_iota(
        jnp.int32, (size, size), 1
    )
    for h in range(heads):
        at = slice(h * width, (h + 1) * width)
        row = running[h : h + 1, :]
        column = columns[:, h : h + 1]
        last = running[h : h + 1, size - 1 :]
        query = query_ref[:, at]
        key_blk = key_ref[:, at]
        value_blk = value_ref[:, at]
        mask = jnp.where(causal, jnp.exp(column - row), 0.0)
        scores = lax.dot_general(
            query, key_blk, (((1,), (1,)), ((), ())), preferred_element_type=jnp.float32
        )
        scores = (scores * mask).astype(jnp.bfloat16)
        state = state_ref[h]
        inner = jnp.dot(scores, value_blk, preferred_element_type=jnp.float32)
        carried = jnp.dot(query, state.astype(jnp.bfloat16), preferred_element_type=jnp.float32)
        out_ref[:, at] = (inner + jnp.exp(column) * carried).astype(jnp.bfloat16)
        state_ref[h] = next_state(state, key_blk, value_blk, column, last)


def norm_kernel(out_ref, gate_ref, gain_ref, result_ref):
    groups, _, width = out_ref.shape
    outs = [out_ref[g].astype(jnp.float32) for g in range(groups)]
    squares = sum(jnp.sum(o * o, axis=1, keepdims=True) for o in outs)
    rstd = lax.rsqrt(squares / (groups * width) + 1e-06)
    for g in range(groups):
        at = slice(g * width, (g + 1) * width)
        gate = gate_ref[g].astype(jnp.float32)
        silu = gate * (1.0 / (1.0 + jnp.exp(-gate)))
        result_ref[:, at] = (silu * outs[g] * rstd * gain_ref[:, at]).astype(jnp.bfloat16)


def local_state(decay_rows, key_rows, values, heads, width):
    rows, local = key_rows.shape
    block = block_of(rows, 256)
    return pl.pallas_call(
        functools.partial(state_kernel, heads=heads, width=width),
        grid=(rows // block,),
        in_specs=[
            pl.BlockSpec((heads, block), lambda i: (0, i)),
            pl.BlockSpec((block, local), lambda i: (i, 0)),
            pl.BlockSpec((block, local), lambda i: (i, 0)),
        ],
        out_specs=[
            pl.BlockSpec((heads, width, width), lambda i: (0, 0, 0)),
            pl.BlockSpec((heads, 128), lambda i: (0, 0)),
        ],
        out_shape=[
            jax.ShapeDtypeStruct((heads, width, width), jnp.float32),
            jax.ShapeDtypeStruct((heads, 128), jnp.float32),
        ],
        name="local_state",
    )(decay_rows, key_rows, values)


def retain(decay_rows, queries, key_rows, values, initial, heads, width):
    rows, local = key_rows.shape
    block = block_of(rows, 256)
    token_spec = pl.BlockSpec((block, local), lambda i: (i, 0))
    return pl.pallas_call(
        functools.partial(retain_kernel, heads=heads, width=width),
        grid=(rows // block,),
        in_specs=[
            pl.BlockSpec((heads, block), lambda i: (0, i)),
            token_spec,
            token_spec,
            token_spec,
            pl.BlockSpec((heads, width, width), lambda i: (0, 0, 0)),
        ],
        out_specs=token_spec,
        out_shape=jax.ShapeDtypeStruct((rows, local), jnp.bfloat16),
        scratch_shapes=[pltpu.VMEM((heads, width, width), jnp.float32)],
        name="retain",
    )(decay_rows, queries, key_rows, values, initial)


def gated_norm(output, gate, gain):
    groups, rows, width = output.shape
    block = block_of(rows, 128)
    piece = pl.BlockSpec((groups, block, width), lambda i: (0, i, 0))
    return pl.pallas_call(
        norm_kernel,
        grid=(rows // block,),
        in_specs=[piece, piece, pl.BlockSpec((1, groups * width), lambda i: (0, 0))],
        out_specs=pl.BlockSpec((block, groups * width), lambda i: (i, 0)),
        out_shape=jax.ShapeDtypeStruct((rows, groups * width), jnp.bfloat16),
        name="gated_norm",
    )(output, gate, gain.reshape(1, -1))


def carried_in(state, total, axis, count):
    decay = jnp.exp(total[:, 0])
    sent = state.astype(jnp.bfloat16)
    incoming = None
    for hop in range(count - 1, 0, -1):
        moves = [(i, i + hop) for i in range(count - hop)]
        arrived = lax.ppermute(sent, axis, moves).astype(jnp.float32)
        if incoming is not None:
            factor = lax.ppermute(decay, axis, moves)
            arrived = arrived + factor[:, None, None] * incoming
        incoming = arrived
    return jnp.zeros_like(state) if incoming is None else incoming


def body(seq_count, mp_count, tokens, w_query, w_key, w_value, w_gate, decay_exponent, forget, norm_gain):
    seq_rows = tokens.shape[0]
    local_width = w_query.shape[1]
    heads = decay_exponent.shape[0]
    width = local_width // heads
    piece = lax.all_gather(tokens, "mp", axis=1, tiled=True)
    rate = jnp.log1p(-jnp.exp2(-decay_exponent.astype(jnp.float32)))
    decay_rows = rate[:, None] - forget.T

    def project(weight):
        return jnp.dot(piece, weight, preferred_element_type=jnp.float32)

    def exchange(source):
        pieces = source.reshape(mp_count, seq_rows // mp_count, local_width)
        return lax.all_to_all(pieces, "mp", split_axis=0, concat_axis=0, tiled=True)

    gate = project(w_gate).astype(jnp.bfloat16)
    moved_gate = exchange(gate)
    key_rows = (project(w_key) * DH ** (-0.5)).astype(jnp.bfloat16)
    values = project(w_value).astype(jnp.bfloat16)
    state, total = local_state(decay_rows, key_rows, values, heads, width)
    incoming = carried_in(state, total, "seq", seq_count)
    queries = project(w_query).astype(jnp.bfloat16)
    output = retain(decay_rows, queries, key_rows, values, incoming, heads, width)
    moved_output = exchange(output)
    return gated_norm(moved_output, moved_gate, norm_gain)


def solution(mesh):
    placed = (
        P(("dp", "seq"), "mp"),
        P(None, "mp"),
        P(None, "mp"),
        P(None, "mp"),
        P(None, "mp"),
        P("mp"),
        P(("dp", "seq"), "mp"),
        P(),
    )
    return jax.shard_map(
        functools.partial(body, mesh.shape["seq"], mesh.shape["mp"]),
        mesh=mesh,
        in_specs=placed,
        out_specs=P(("dp", "seq", "mp"), None),
        check_vma=False,
    )
```

time: 341 us -> 186 us (0.55)
  local copies, waits for them, and re-layouts: 131 us -> 0.2 us
  Pallas kernels: 0 us -> 31 us
  matrix products: 67.6 us -> 38 us
  other arithmetic: 25.1 us -> 2.39 us
  blocking collectives: 10.7 us -> 30.1 us
  waiting for transfers between devices: 80.8 us -> 62.5 us
    dynamic_update_slice x8 -> x0, local copies, waits for them, and re-layouts: 88.5 us -> none  [run_blocks(): lax.scan(advance, initial, (shaped(queries), shaped(key_rows), shaped(val...]
    pallas_call x0 -> x3, Pallas kernels: none -> 31 us  [the longest x1 15.3 us: retain(): pl.pallas_call(functools.partial(retain_kernel, heads=heads, width=width)...]
    all_to_all x0 -> x1, blocking collectives: none -> 30.1 us  [exchange(): return lax.all_to_all(pieces, 'mp', split_axis=0, concat_axis=0, tiled=True)]
    dot_general x17 -> x4, matrix products: 67.6 us -> 38 us  [project(): return jnp.dot(piece, weight, preferred_element_type=jnp.float32)]
    all_to_all x2 -> x1, waiting for transfers between devices: 20.9 us -> 0.01 us  [exchange(): return lax.all_to_all(pieces, 'mp', split_axis=0, concat_axis=0, tiled=True)]
    reshape x8 -> x0, local copies, waits for them, and re-layouts: 14.2 us -> none  [the longest x3 8.09 us: shaped(): return source.reshape(block_count, block_rows, head_count, head_width)]
    dynamic_slice x8 -> x0, local copies, waits for them, and re-layouts: 11.9 us -> none  [run_blocks(): lax.scan(advance, initial, (shaped(queries), shaped(key_rows), shaped(val...]
    convert_element_type x2 -> x0, local copies, waits for them, and re-layouts: 7.99 us -> none  [the longest x1 5.41 us: body(): output_float = moved_output.astype(jnp.float32)]
  transfers between devices with their start and end apart: 3 -> 3, of which waited for: 2 -> 1; matrix products, arithmetic and copies ran while one was open for 7% -> 17% of each run, Pallas kernels for 0% -> 14%
where the time goes in v1:
time: 186 us
  waiting for transfers between devices  62.5 us (34%)
  matrix products  38 us (20%)
  Pallas kernels  31 us (17%)
  blocking collectives  30.1 us (16%)
  between operations  13.4 us (7%)
  starting transfers between devices  8.06 us (4%)
  other arithmetic  2.39 us (1%)
    all_gather x1, waiting for transfers between devices, body(): piece = lax.all_gather(tokens, 'mp', axis=1, tiled=True)  61.8 us
    dot_general x4, matrix products, project(): return jnp.dot(piece, weight, preferred_element_type=jnp.float32)  38 us
    all_to_all x1, blocking collectives, exchange(): return lax.all_to_all(pieces, 'mp', split_axis=0, concat_axis=0, tiled=True)  30.1 us
    pallas_call x1, Pallas kernels, retain(): pl.pallas_call(functools.partial(retain_kernel, heads=heads, width=width)...  15.3 us
    pallas_call x1, Pallas kernels, local_state(): pl.pallas_call(functools.partial(state_kernel, heads=heads, width=width),...  10.7 us
    pallas_call x1, Pallas kernels, gated_norm(): pl.pallas_call(norm_kernel, grid=(rows // block,), in_specs=[piece, piece...  5.06 us
    all_to_all x1, starting transfers between devices, exchange(): return lax.all_to_all(pieces, 'mp', split_axis=0, concat_axis=0, tiled=True)  4.49 us
  transfers between devices with their start and end apart: 3, of which 1 were waited for; matrix products, arithmetic and copies ran while one was open for 17% of the time, Pallas kernels for 14%

profile of v1, /device:TPU:0, one launch (start us, length us, event | category | flops | bytes accessed | tf_op | source)
XLA Modules:
  0.0 185.7 jit_solution(449358468284497534)
XLA Ops:
  6.5 0.0 copy-start
  6.5 0.0 copy-start.3
  6.5 0.0 copy-start.1
  6.5 0.0 all-gather.2.cloned.1.call-start
  6.5 0.7 all-gather.2.cloned.1.call-update
  7.3 0.1 copy-done.3
  7.4 0.1 copy-done.1
  7.5 0.7 subtract_bitcast_fusion.decay_ref
  8.2 61.8 %all-gather.2.cloned.1.call-done = bf16[2048,2048]{1,0:T(8,128)(2,1)} async-done(((bf16[2048,512]{1,0:T(8,128)(2,1)}), bf16[2048,2048]{1,0:T(8,128)(2,1)}) %all-gather.2.cloned.1.call-update) | async-done | bytes 8388624 | tf_op jit(solution)/shard_map/all_gather | solution.py:178
  69.9 0.0 copy-done
  69.9 9.1 %convolution_convert_fusion = bf16[2048,512]{1,0:T(8,128)(2,1)} fusion(bf16[2048,2048]{1,0:T(8,128)(2,1)} %all-gather.2.cloned.1.call-done, bf16[2048,512]{1,0:T(8,128)(2,1)S(1)} %copy-done), kind=kOutput, calls=%fused_computation.1 | convolution fusion | flops 4296015872 | bytes 12582912 | tf_op jit(solution)/shard_map/dot_general | solution.py:183
  79.0 4.5 %all-to-all-start.1 = ((bf16[4,512,512]{2,1,0:T(8,128)(2,1)}), bf16[4,512,512]{2,1,0:T(8,128)(2,1)}, u32[]{:S(2)}, u32[]{:S(2)}) async-start(bf16[4,512,512]{2,1,0:T(8,128)(2,1)} %bitcast.14), calls=%async_computation.1 | async-start | bytes 4194304 | tf_op jit(solution)/shard_map/all_to_all | solution.py:187
  83.5 0.0 copy-start.2
  83.6 9.9 %convolution_convert_fusion.1.value_ref = bf16[2048,512]{1,0:T(8,128)(2,1)} fusion(bf16[2048,2048]{1,0:T(8,128)(2,1)} %all-gather.2.cloned.1.call-done, bf16[2048,512]{1,0:T(8,128)(2,1)} %param.11), kind=kOutput, calls=%fused_computation.2 | convolution fusion | flops 4296015872 | bytes 12582912 | tf_op jit(solution)/shard_map/dot_general | solution.py:183
  93.5 0.0 copy-done.2
  93.5 9.1 %multiply_convert_fusion.key_ref = bf16[2048,512]{1,0:T(8,128)(2,1)} fusion(bf16[2048,2048]{1,0:T(8,128)(2,1)} %all-gather.2.cloned.1.call-done, bf16[2048,512]{1,0:T(8,128)(2,1)S(1)} %copy-done.2), kind=kOutput, calls=%fused_computation | convolution fusion | flops 4297064448 | bytes 12582912 | tf_op jit(solution)/shard_map/dot_general | solution.py:183
  102.6 10.7 %local_state.1 = (f32[4,128,128]{2,1,0:T(8,128)}, f32[4,128]{1,0:T(4,128)}) custom-call(f32[4,2048]{1,0:T(4,128)} %subtract_bitcast_fusion.decay_ref, bf16[2048,512]{1,0:T(8,128)(2,1)} %multiply_convert_fusion.key_ref, bf16[2048,512]{1,0:T(8,128)(2,1)} %convolution_convert_fusion.1.value_ref), custom_call_target="tpu_custom_call" | custom-call | tf_op jit(solution)/shard_map/local_state/pallas_call | solution.py:104
  113.3 1.0 convert_element_type.25
  114.3 3.6 %collective-permute-start = (bf16[4,128,128]{2,1,0:T(8,128)(2,1)S(1)}, bf16[4,128,128]{2,1,0:T(8,128)(2,1)S(1)}, u32[]{:S(2)}, u32[]{:S(2)}) collective-permute-start(bf16[4,128,128]{2,1,0:T(8,128)(2,1)S(1)} %convert_element_type.25), channel_id=1, source_target_pairs={{0,16},{1,17},{2,18},{3,19},{4,20},{5,21},{6,22},{7,23},{8,24},{9,... | collective-permute-start | bytes 393224 | tf_op jit(solution)/shard_map/ppermute | solution.py:165
  117.8 9.8 %convolution_convert_fusion.2.query_ref = bf16[2048,512]{1,0:T(8,128)(2,1)} fusion(bf16[2048,2048]{1,0:T(8,128)(2,1)} %all-gather.2.cloned.1.call-done, bf16[2048,512]{1,0:T(8,128)(2,1)} %param.9), kind=kOutput, calls=%fused_computation.3 | convolution fusion | flops 4296015872 | bytes 12582912 | tf_op jit(solution)/shard_map/dot_general | solution.py:183
  127.6 0.0 collective-permute-done
  127.7 0.7 convert_element_type.26.initial_ref
  128.4 15.3 %retain.1 = bf16[2048,512]{1,0:T(8,128)(2,1)} custom-call(f32[4,2048]{1,0:T(4,128)} %subtract_bitcast_fusion.decay_ref, bf16[2048,512]{1,0:T(8,128)(2,1)} %convolution_convert_fusion.2.query_ref, bf16[2048,512]{1,0:T(8,128)(2,1)} %multiply_convert_fusion.key_ref, bf16[2048,512]{1,0:T(8,128)(2,1)} %convolution_convert_fusion.1.value_ref, ...), custom_call_target="tpu_custom_call" | custom-call | tf_op jit(solution)/shard_map/retain/pallas_call | solution.py:128
  143.6 0.0 all-to-all-done.1.gate_ref
  143.6 30.1 %all_to_all.10.out_ref = bf16[4,512,512]{2,1,0:T(8,128)(2,1)} all-to-all(bf16[4,512,512]{2,1,0:T(8,128)(2,1)} %bitcast.13), channel_id=1, replica_groups=mesh['seq'=2,'mp'=4,'dp'=4] {'mp'}, dimensions={0} | all-to-all | bytes 4194304 | tf_op jit(solution)/shard_map/all_to_all | solution.py:187
  173.8 5.1 %gated_norm.1 = bf16[512,2048]{1,0:T(8,128)(2,1)} custom-call(bf16[4,512,512]{2,1,0:T(8,128)(2,1)} %all_to_all.10.out_ref, bf16[4,512,512]{2,1,0:T(8,128)(2,1)} %all-to-all-done.1.gate_ref, f32[1,2048]{1,0:T(1,128)} %bitcast.15), custom_call_target="tpu_custom_call" | custom-call | tf_op jit(solution)/shard_map/gated_norm/pallas_call | solution.py:149
  (1 shorter events, 0.0 us)
Async XLA Ops:
  6.5 63.4 %copy-start = (bf16[2048,512]{1,0:T(8,128)(2,1)S(1)}, bf16[2048,512]{1,0:T(8,128)(2,1)}, u32[]{:S(2)}) copy-start(bf16[2048,512]{1,0:T(8,128)(2,1)} %param.12) | copy-start | bytes 6291460
  6.5 0.8 copy-start.3
  6.5 0.9 copy-start.1
  6.5 63.4 %all-gather.2.cloned.1.call-start = ((), (), s32[]{:S(2)}) async-start(), calls=%async_computation.2 | async-start | bytes 10485760 | tf_op jit(solution)/shard_map/all_gather | solution.py:178
  79.0 64.6 %all-to-all-start.1 = ((bf16[4,512,512]{2,1,0:T(8,128)(2,1)}), bf16[4,512,512]{2,1,0:T(8,128)(2,1)}, u32[]{:S(2)}, u32[]{:S(2)}) async-start(bf16[4,512,512]{2,1,0:T(8,128)(2,1)} %bitcast.14), calls=%async_computation.1 | async-start | bytes 4194304 | tf_op jit(solution)/shard_map/all_to_all | solution.py:187
  83.5 10.0 %copy-start.2 = (bf16[2048,512]{1,0:T(8,128)(2,1)S(1)}, bf16[2048,512]{1,0:T(8,128)(2,1)}, u32[]{:S(2)}) copy-start(bf16[2048,512]{1,0:T(8,128)(2,1)} %param.10) | copy-start | bytes 6291460
  114.3 13.4 %collective-permute-start = (bf16[4,128,128]{2,1,0:T(8,128)(2,1)S(1)}, bf16[4,128,128]{2,1,0:T(8,128)(2,1)S(1)}, u32[]{:S(2)}, u32[]{:S(2)}) collective-permute-start(bf16[4,128,128]{2,1,0:T(8,128)(2,1)S(1)} %convert_element_type.25), channel_id=1, source_target_pairs={{0,16},{1,17},{2,18},{3,19},{4,20},{5,21},{6,22},{7,23},{8,24},{9,... | collective-permute-start | bytes 393224 | tf_op jit(solution)/shard_map/ppermute | solution.py:165
Sparse Core Ops, SparseCore 0:
  8.9 60.9 all-gather.1
